TPU v7x, 8 devices: a whole 2x2x1 slice. The times are simulated.
8 devices in a mesh: dp: 2 (over z, y), fsdp: 4 (over x, core).
Axes of the slice: x: 2, y: 2, z: 1, core: 2. Of those that a mesh axis runs over, the one named last changes fastest.
Arguments:
- h_saved: bfloat16 [4, 16, 2048, 896], P(None, ('dp', 'fsdp'))
- grad_out: bfloat16 [16, 2048, 896], P(('dp', 'fsdp'))
- w_gate: bfloat16 [4, 896, 4864], P(None, 'fsdp')
- w_up: bfloat16 [4, 896, 4864], P(None, 'fsdp')
- w_down: bfloat16 [4, 4864, 896], P(None, 'fsdp')
Outputs:
- output 1: float32 [4, 896, 4864], P(None, 'fsdp')
- output 2: float32 [4, 896, 4864], P(None, 'fsdp')
- output 3: float32 [4, 4864, 896], P(None, 'fsdp')
- output 4: bfloat16 [16, 2048, 896], P(('dp', 'fsdp'))
All inputs are finite; a program needn't handle non-finite values.
Results may differ from a plain program's by a relative error of at most 0.00808875.
Values are sent between devices in bfloat16 or wider.
A program may use at most 1 GiB of HBM per device.

v0:
```python
import jax
import jax.numpy as jnp
from jax import lax
from jax.sharding import PartitionSpec as P

EPS = 1e-5


def layer_backward(h_in, g_acc, gate_w, up_w, down_w):
    x_full = h_in.astype(jnp.float32)
    inv_rms = lax.rsqrt(jnp.mean(x_full * x_full, axis=-1, keepdims=True) + EPS)
    norm_f = x_full * inv_rms
    norm_b = norm_f.astype(jnp.bfloat16)
    pre_gate = jnp.einsum("td,df->tf", norm_b, gate_w, preferred_element_type=jnp.float32)
    pre_up = jnp.einsum("td,df->tf", norm_b, up_w, preferred_element_type=jnp.float32)
    sig_gate = jax.nn.sigmoid(pre_gate)
    silu_gate = pre_gate * sig_gate
    act_b = (silu_gate * pre_up).astype(jnp.bfloat16)
    g_bf = g_acc.astype(jnp.bfloat16)
    d_act = jnp.einsum("td,fd->tf", g_bf, down_w, preferred_element_type=jnp.float32)
    grad_down = jnp.einsum("tf,td->fd", act_b, g_bf, preferred_element_type=jnp.float32)
    d_gate_b = (d_act * pre_up * sig_gate * (1.0 + pre_gate * (1.0 - sig_gate))).astype(jnp.bfloat16)
    d_up_b = (d_act * silu_gate).astype(jnp.bfloat16)
    grad_gate = jnp.einsum("td,tf->df", norm_b, d_gate_b, preferred_element_type=jnp.float32)
    grad_up = jnp.einsum("td,tf->df", norm_b, d_up_b, preferred_element_type=jnp.float32)
    d_norm = jnp.einsum("tf,df->td", d_gate_b, gate_w, preferred_element_type=jnp.float32) + jnp.einsum("tf,df->td", d_up_b, up_w, preferred_element_type=jnp.float32)
    d_x = inv_rms * (d_norm - norm_f * jnp.mean(d_norm * norm_f, axis=-1, keepdims=True))
    return g_acc + d_x, grad_gate, grad_up, grad_down


def reduce_grad(local_grad):
    shard_sum = lax.psum_scatter(local_grad, "fsdp", scatter_dimension=0, tiled=True)
    return lax.psum(shard_sum, "dp")


def solution(mesh):
    tok_spec = P(("dp", "fsdp"))
    stack_spec = P(None, ("dp", "fsdp"))
    weight_spec = P(None, "fsdp")

    def local_backward(h_saved, grad_out, gate_sh, up_sh, down_sh):
        n_layers = h_saved.shape[0]
        b_loc, seq_len, model_width = grad_out.shape
        tokens = b_loc * seq_len
        g_acc = grad_out.reshape(tokens, model_width).astype(jnp.float32)
        gate_parts = []
        up_parts = []
        down_parts = []
        for layer_idx in reversed(range(n_layers)):
            gate_w = lax.all_gather(gate_sh[layer_idx], "fsdp", axis=0, tiled=True)
            up_w = lax.all_gather(up_sh[layer_idx], "fsdp", axis=0, tiled=True)
            down_w = lax.all_gather(down_sh[layer_idx], "fsdp", axis=0, tiled=True)
            h_in = h_saved[layer_idx].reshape(tokens, model_width)
            g_acc, grad_gate, grad_up, grad_down = layer_backward(h_in, g_acc, gate_w, up_w, down_w)
            gate_parts.append(reduce_grad(grad_gate))
            up_parts.append(reduce_grad(grad_up))
            down_parts.append(reduce_grad(grad_down))
        d_h0 = g_acc.reshape(b_loc, seq_len, model_width).astype(jnp.bfloat16)
        return jnp.stack(gate_parts[::-1]), jnp.stack(up_parts[::-1]), jnp.stack(down_parts[::-1]), d_h0

    return jax.shard_map(local_backward, mesh=mesh, in_specs=(stack_spec, tok_spec, weight_spec, weight_spec, weight_spec), out_specs=(weight_spec, weight_spec, weight_spec, tok_spec), check_vma=False)
```

profile of v0, /device:TPU:0, one launch (start us, length us, event | category | flops | bytes accessed | tf_op | source)
XLA Modules:
  0.0 3408.3 jit_solution(5742836744377812068)
XLA Ops:
  133.8 50.3 %fusion.57 = f32[4096,4864]{1,0:T(8,128)} fusion(bf16[4096,896]{1,0:T(8,128)(2,1)} %fusion.13, bf16[1,896,4864]{2,1,0:T(8,128)(2,1)} %all-gather.29.cloned.1.call-done), kind=kOutput, calls=%fused_computation.82 | convolution fusion | flops 35701915648 | bytes 95748096 | tf_op jit(solution)/shard_map/td,df->tf/dot_general | solution.py:14
  184.0 65.1 %fusion.7 = f32[4864,896]{1,0:T(8,128)} fusion(bf16[4096,896]{1,0:T(8,128)(2,1)} %bitcast.172, f32[4096,4864]{1,0:T(8,128)} %fusion.64, f32[4096,4864]{1,0:T(8,128)} %fusion.57), kind=kOutput, calls=%fused_computation.23 | convolution fusion | flops 35821453312 | bytes 184156160 | tf_op jit(solution)/shard_map/tf,td->fd/dot_general | solution.py:21
  249.2 96.3 %multiply_convert_fusion.10 = (bf16[4096,4864]{1,0:T(8,128)(2,1)}, bf16[4096,4864]{1,0:T(8,128)(2,1)}) fusion(f32[4096,4864]{1,0:T(8,128)} %fusion.57, f32[4096,4864]{1,0:T(8,128)} %fusion.64, bf16[4096,896]{1,0:T(8,128)(2,1)} %bitcast.173, bf16[1,4864,896]{2,1,0:T(8,128)(2,1)} %all-gather.25.cloned.1.call-done), kind=kOutput, calls=%fused_computation.16 | convolution fusion | flops 35960913920 | bytes 255131648 | tf_op jit(solution)/shard_map/td,fd->tf/dot_general | solution.py:20
  345.5 55.4 %fusion.84 = f32[896,4864]{1,0:T(8,128)} fusion(bf16[4096,896]{1,0:T(8,128)(2,1)} %fusion.13, bf16[4096,4864]{1,0:T(8,128)(2,1)} %get-tuple-element.27), kind=kOutput, calls=%fused_computation.115 | convolution fusion | flops 35701915648 | bytes 64618496 | tf_op jit(solution)/shard_map/td,tf->df/dot_general | solution.py:24
  449.3 50.6 %fusion.62 = f32[4096,896]{1,0:T(8,128)} fusion(bf16[4096,4864]{1,0:T(8,128)(2,1)} %get-tuple-element.26, bf16[1,896,4864]{2,1,0:T(8,128)(2,1)} %all-gather.27.cloned.1.call-done), kind=kOutput, calls=%fused_computation.85 | convolution fusion | flops 35701915648 | bytes 63242240 | tf_op jit(solution)/shard_map/tf,df->td/dot_general | solution.py:26
  499.9 51.2 %multiply_reduce_fusion.5 = (f32[4096]{0:T(1024)S(1)}, f32[4096,896]{1,0:T(8,128)}) fusion(f32[4096]{0:T(1024)S(1)} %bitcast.200, bf16[4,2,2048,896]{3,2,1,0:T(8,128)(2,1)} %param.5, f32[4096,896]{1,0:T(8,128)} %fusion.62, bf16[4096,4864]{1,0:T(8,128)(2,1)} %get-tuple-element.27, bf16[1,896,4864]{2,1,0:T(8,128)(2,1)} %all-gather.29.cloned.1.call-done), kind=kOutput, calls=%fused_computation.40 | convolution fusion | flops 35720261632 | bytes 85295104 | tf_op jit(solution)/shard_map/tf,df->td/dot_general | solution.py:26
  568.0 50.4 %fusion.44 = f32[4096,4864]{1,0:T(8,128)} fusion(bf16[4096,896]{1,0:T(8,128)(2,1)} %get-tuple-element.33, bf16[1,896,4864]{2,1,0:T(8,128)(2,1)} %all-gather.35.cloned.1.call-done), kind=kOutput, calls=%fused_computation.71 | convolution fusion | flops 35701915648 | bytes 95748096 | tf_op jit(solution)/shard_map/td,df->tf/dot_general | solution.py:14
  668.7 71.7 %fusion.6 = f32[4864,896]{1,0:T(8,128)} fusion(f32[4096,4864]{1,0:T(8,128)} %fusion.51, f32[4096,4864]{1,0:T(8,128)} %fusion.44, f32[4096,896]{1,0:T(8,128)} %get-tuple-element.32), kind=kOutput, calls=%fused_computation.22 | convolution fusion | flops 35825123328 | bytes 191496192 | tf_op jit(solution)/shard_map/tf,td->fd/dot_general | solution.py:21
  740.5 97.7 %multiply_convert_fusion.8 = (bf16[4096,4864]{1,0:T(8,128)(2,1)}, bf16[4096,4864]{1,0:T(8,128)(2,1)}) fusion(f32[4096,4864]{1,0:T(8,128)} %fusion.44, f32[4096,4864]{1,0:T(8,128)} %fusion.51, bf16[1,4864,896]{2,1,0:T(8,128)(2,1)} %all-gather.31.cloned.1.call-done, f32[4096,896]{1,0:T(8,128)} %get-tuple-element.32), kind=kOutput, calls=%fused_computation.12 | convolution fusion | flops 35964583936 | bytes 262471680 | tf_op jit(solution)/shard_map/td,fd->tf/dot_general | solution.py:20
  982.6 51.1 %multiply_reduce_fusion.3 = (f32[4096]{0:T(1024)S(1)}, f32[4096,896]{1,0:T(8,128)}) fusion(f32[4096]{0:T(1024)S(1)} %bitcast.206, bf16[4,2,2048,896]{3,2,1,0:T(8,128)(2,1)} %param.5, f32[4096,896]{1,0:T(8,128)} %fusion.49, bf16[4096,4864]{1,0:T(8,128)(2,1)} %get-tuple-element.25, bf16[1,896,4864]{2,1,0:T(8,128)(2,1)} %all-gather.35.cloned.1.call-done), kind=kOutput, calls=%fused_computation.37 | convolution fusion | flops 35720261632 | bytes 85295104 | tf_op jit(solution)/shard_map/tf,df->td/dot_general | solution.py:26
  1057.0 50.5 %fusion.31 = f32[4096,4864]{1,0:T(8,128)} fusion(bf16[4096,896]{1,0:T(8,128)(2,1)} %get-tuple-element.31, bf16[1,896,4864]{2,1,0:T(8,128)(2,1)} %all-gather.41.cloned.1.call-done), kind=kOutput, calls=%fused_computation.60 | convolution fusion | flops 35701915648 | bytes 95748096 | tf_op jit(solution)/shard_map/td,df->tf/dot_general | solution.py:14
  1157.7 71.6 %fusion.5 = f32[4864,896]{1,0:T(8,128)} fusion(f32[4096,4864]{1,0:T(8,128)} %fusion.38, f32[4096,4864]{1,0:T(8,128)} %fusion.31, f32[4096,896]{1,0:T(8,128)} %get-tuple-element.30), kind=kOutput, calls=%fused_computation.21 | convolution fusion | flops 35825123328 | bytes 191496192 | tf_op jit(solution)/shard_map/tf,td->fd/dot_general | solution.py:21
  1229.4 97.9 %multiply_convert_fusion.6 = (bf16[4096,4864]{1,0:T(8,128)(2,1)}, bf16[4096,4864]{1,0:T(8,128)(2,1)}) fusion(f32[4096,4864]{1,0:T(8,128)} %fusion.31, f32[4096,4864]{1,0:T(8,128)} %fusion.38, bf16[1,4864,896]{2,1,0:T(8,128)(2,1)} %all-gather.37.cloned.1.call-done, f32[4096,896]{1,0:T(8,128)} %get-tuple-element.30), kind=kOutput, calls=%fused_computation.8 | convolution fusion | flops 35964583936 | bytes 262471680 | tf_op jit(solution)/shard_map/td,fd->tf/dot_general | solution.py:20
  1471.6 51.1 %multiply_reduce_fusion.1 = (f32[4096]{0:T(1024)S(1)}, f32[4096,896]{1,0:T(8,128)}) fusion(f32[4096]{0:T(1024)S(1)} %bitcast.203, bf16[4,2,2048,896]{3,2,1,0:T(8,128)(2,1)} %param.5, f32[4096,896]{1,0:T(8,128)} %fusion.36, bf16[4096,4864]{1,0:T(8,128)(2,1)} %get-tuple-element.23, bf16[1,896,4864]{2,1,0:T(8,128)(2,1)} %all-gather.41.cloned.1.call-done), kind=kOutput, calls=%fused_computation.34 | convolution fusion | flops 35720261632 | bytes 85295104 | tf_op jit(solution)/shard_map/tf,df->td/dot_general | solution.py:26
  1546.0 50.7 %fusion.18 = f32[4096,4864]{1,0:T(8,128)} fusion(bf16[4096,896]{1,0:T(8,128)(2,1)} %get-tuple-element.29, bf16[1,896,4864]{2,1,0:T(8,128)(2,1)} %all-gather.47.cloned.1.call-done), kind=kOutput, calls=%fused_computation.49 | convolution fusion | flops 35701915648 | bytes 95748096 | tf_op jit(solution)/shard_map/td,df->tf/dot_general | solution.py:14
  1596.6 50.2 %fusion.25 = f32[4096,4864]{1,0:T(8,128)} fusion(bf16[4096,896]{1,0:T(8,128)(2,1)} %get-tuple-element.29, bf16[1,896,4864]{2,1,0:T(8,128)(2,1)} %all-gather.45.cloned.1.call-done), kind=kOutput, calls=%fused_computation.54 | convolution fusion | flops 35701915648 | bytes 95748096 | tf_op jit(solution)/shard_map/td,df->tf/dot_general | solution.py:15
  1646.8 71.5 %fusion.4 = f32[4864,896]{1,0:T(8,128)} fusion(f32[4096,4864]{1,0:T(8,128)} %fusion.25, f32[4096,4864]{1,0:T(8,128)} %fusion.18, f32[4096,896]{1,0:T(8,128)} %get-tuple-element.28), kind=kOutput, calls=%fused_computation.20 | convolution fusion | flops 35825123328 | bytes 191496192 | tf_op jit(solution)/shard_map/tf,td->fd/dot_general | solution.py:21
  1718.5 97.7 %multiply_convert_fusion.4 = (bf16[4096,4864]{1,0:T(8,128)(2,1)}, bf16[4096,4864]{1,0:T(8,128)(2,1)}) fusion(f32[4096,4864]{1,0:T(8,128)} %fusion.18, f32[4096,4864]{1,0:T(8,128)} %fusion.25, bf16[1,4864,896]{2,1,0:T(8,128)(2,1)} %all-gather.43.cloned.1.call-done, f32[4096,896]{1,0:T(8,128)} %get-tuple-element.28), kind=kOutput, calls=%fused_computation.4 | convolution fusion | flops 35964583936 | bytes 262471680 | tf_op jit(solution)/shard_map/td,fd->tf/dot_general | solution.py:20
  1909.3 69.8 %reduce-scatter.29.cloned.1.call-done = f32[1216,896]{1,0:T(8,128)} async-done(((f32[4864,896]{1,0:T(8,128)}), f32[1216,896]{1,0:T(8,128)}) %reduce-scatter.29.cloned.1.call-update) | async-done | bytes 4358160 | tf_op jit(solution)/shard_map/reduce_scatter | solution.py:32
  1979.1 125.3 %reduce-scatter.13.cloned.1.call-done = f32[224,4864]{1,0:T(8,128)} async-done(((f32[896,4864]{1,0:T(8,128)}), f32[224,4864]{1,0:T(8,128)}) %reduce-scatter.13.cloned.1.call-update) | async-done | bytes 4358160 | tf_op jit(solution)/shard_map/reduce_scatter | solution.py:32
  2104.5 125.1 %reduce-scatter.21.cloned.1.call-done = f32[224,4864]{1,0:T(8,128)} async-done(((f32[896,4864]{1,0:T(8,128)}), f32[224,4864]{1,0:T(8,128)}) %reduce-scatter.21.cloned.1.call-update) | async-done | bytes 4358160 | tf_op jit(solution)/shard_map/reduce_scatter | solution.py:32
  2229.6 50.2 %fusion.23 = f32[4096,896]{1,0:T(8,128)} fusion(bf16[4096,4864]{1,0:T(8,128)(2,1)} %get-tuple-element.20, bf16[1,896,4864]{2,1,0:T(8,128)(2,1)} %all-gather.45.cloned.1.call-done), kind=kOutput, calls=%fused_computation.52 | convolution fusion | flops 35701915648 | bytes 63242240 | tf_op jit(solution)/shard_map/tf,df->td/dot_general | solution.py:26
  2279.9 51.1 %multiply_reduce_fusion = (f32[4096]{0:T(1024)S(1)}, f32[4096,896]{1,0:T(8,128)}) fusion(f32[4096]{0:T(1024)S(1)} %bitcast.197, bf16[4,2,2048,896]{3,2,1,0:T(8,128)(2,1)} %param.5, f32[4096,896]{1,0:T(8,128)} %fusion.23, bf16[4096,4864]{1,0:T(8,128)(2,1)} %get-tuple-element.21, bf16[1,896,4864]{2,1,0:T(8,128)(2,1)} %all-gather.47.cloned.1.call-done), kind=kOutput, calls=%fused_computation.32 | convolution fusion | flops 35720261632 | bytes 85295104 | tf_op jit(solution)/shard_map/tf,df->td/dot_general | solution.py:26
  2346.6 1020.2 %all-reduce.3.cloned.1.call-done = (f32[1,224,4864]{2,1,0:T(8,128)}, f32[1,224,4864]{2,1,0:T(8,128)}, f32[1,224,4864]{2,1,0:T(8,128)}, f32[1,224,4864]{2,1,0:T(8...) async-done(((f32[1,224,4864]{2,1,0:T(8,128)}, ...) | async-done | bytes 52297744 | tf_op jit(solution)/shard_map/psum | solution.py:33
  (162 shorter events, 770.8 us)
Async XLA Ops:
  13.4 120.3 %all-gather.29.cloned.1.call-start = ((), (), s32[]{:S(2)}) async-start(), calls=%async_computation.26 | async-start | bytes 10895360 | tf_op jit(solution)/shard_map/all_gather | solution.py:50
  19.7 229.5 %all-gather.25.cloned.1.call-start = ((), (), s32[]{:S(2)}) async-start(), calls=%async_computation.24 | async-start | bytes 10895360 | tf_op jit(solution)/shard_map/all_gather | solution.py:52
  26.0 542.1 %all-gather.35.cloned.1.call-start = ((), (), s32[]{:S(2)}) async-start(), calls=%async_computation.29 | async-start | bytes 10895360 | tf_op jit(solution)/shard_map/all_gather | solution.py:50
  26.5 591.9 %all-gather.33.cloned.1.call-start = ((), (), s32[]{:S(2)}) async-start(), calls=%async_computation.28 | async-start | bytes 10895360 | tf_op jit(solution)/shard_map/all_gather | solution.py:51
  27.1 713.3 %all-gather.31.cloned.1.call-start = ((), (), s32[]{:S(2)}) async-start(), calls=%async_computation.27 | async-start | bytes 10895360 | tf_op jit(solution)/shard_map/all_gather | solution.py:52
  27.7 1029.3 %all-gather.41.cloned.1.call-start = ((), (), s32[]{:S(2)}) async-start(), calls=%async_computation.32 | async-start | bytes 10895360 | tf_op jit(solution)/shard_map/all_gather | solution.py:50
  28.5 1079.0 %all-gather.39.cloned.1.call-start = ((), (), s32[]{:S(2)}) async-start(), calls=%async_computation.31 | async-start | bytes 10895360 | tf_op jit(solution)/shard_map/all_gather | solution.py:51
  29.2 1200.2 %all-gather.37.cloned.1.call-start = ((), (), s32[]{:S(2)}) async-start(), calls=%async_computation.30 | async-start | bytes 10895360 | tf_op jit(solution)/shard_map/all_gather | solution.py:52
  29.9 1516.0 %all-gather.47.cloned.1.call-start = ((), (), s32[]{:S(2)}) async-start(), calls=%async_computation.35 | async-start | bytes 10895360 | tf_op jit(solution)/shard_map/all_gather | solution.py:50
  30.5 1566.1 %all-gather.45.cloned.1.call-start = ((), (), s32[]{:S(2)}) async-start(), calls=%async_computation.34 | async-start | bytes 10895360 | tf_op jit(solution)/shard_map/all_gather | solution.py:51
  31.3 1687.2 %all-gather.43.cloned.1.call-start = ((), (), s32[]{:S(2)}) async-start(), calls=%async_computation.33 | async-start | bytes 10895360 | tf_op jit(solution)/shard_map/all_gather | solution.py:52
  31.8 1877.3 %reduce-scatter.35.cloned.1.call-start = ((), (), s32[]{:S(2)}) async-start(), calls=%async_computation.23 | async-start | bytes 21790720 | tf_op jit(solution)/shard_map/reduce_scatter | solution.py:32
  249.1 1660.0 %reduce-scatter.19.cloned.1.call-start = ((), (), s32[]{:S(2)}) async-start(), calls=%async_computation.15 | async-start | bytes 21790720 | tf_op jit(solution)/shard_map/reduce_scatter | solution.py:32
  400.9 1508.3 %reduce-scatter.27.cloned.1.call-start = ((), (), s32[]{:S(2)}) async-start(), calls=%async_computation.19 | async-start | bytes 21790720 | tf_op jit(solution)/shard_map/reduce_scatter | solution.py:32
  449.2 1460.0 %reduce-scatter.33.cloned.1.call-start = ((), (), s32[]{:S(2)}) async-start(), calls=%async_computation.22 | async-start | bytes 21790720 | tf_op jit(solution)/shard_map/reduce_scatter | solution.py:32
  740.4 1168.8 %reduce-scatter.17.cloned.1.call-start = ((), (), s32[]{:S(2)}) async-start(), calls=%async_computation.14 | async-start | bytes 21790720 | tf_op jit(solution)/shard_map/reduce_scatter | solution.py:32
  884.4 1024.8 %reduce-scatter.25.cloned.1.call-start = ((), (), s32[]{:S(2)}) async-start(), calls=%async_computation.18 | async-start | bytes 21790720 | tf_op jit(solution)/shard_map/reduce_scatter | solution.py:32
  932.5 976.8 %reduce-scatter.31.cloned.1.call-start = ((), (), s32[]{:S(2)}) async-start(), calls=%async_computation.21 | async-start | bytes 21790720 | tf_op jit(solution)/shard_map/reduce_scatter | solution.py:32
  1229.3 680.0 %reduce-scatter.15.cloned.1.call-start = ((), (), s32[]{:S(2)}) async-start(), calls=%async_computation.13 | async-start | bytes 21790720 | tf_op jit(solution)/shard_map/reduce_scatter | solution.py:32
  1373.5 535.8 %reduce-scatter.23.cloned.1.call-start = ((), (), s32[]{:S(2)}) async-start(), calls=%async_computation.17 | async-start | bytes 21790720 | tf_op jit(solution)/shard_map/reduce_scatter | solution.py:32
  1421.3 557.8 %reduce-scatter.29.cloned.1.call-start = ((), (), s32[]{:S(2)}) async-start(), calls=%async_computation.20 | async-start | bytes 21790720 | tf_op jit(solution)/shard_map/reduce_scatter | solution.py:32
  1718.4 386.1 %reduce-scatter.13.cloned.1.call-start = ((), (), s32[]{:S(2)}) async-start(), calls=%async_computation.12 | async-start | bytes 21790720 | tf_op jit(solution)/shard_map/reduce_scatter | solution.py:32
  1862.4 367.2 %reduce-scatter.21.cloned.1.call-start = ((), (), s32[]{:S(2)}) async-start(), calls=%async_computation.16 | async-start | bytes 21790720 | tf_op jit(solution)/shard_map/reduce_scatter | solution.py:32
  1909.1 1457.7 %all-reduce.3.cloned.1.call-start = ((), (), s32[]{:S(2)}) async-start(), calls=%async_computation.36 | async-start | bytes 104595456 | tf_op jit(solution)/shard_map/psum | solution.py:33
  (27 other events, 788.6 us)
Sparse Core Ops, SparseCore 0:
  13.5 60.4 all-gather.26
  76.1 57.6 all-gather.28
  135.9 57.6 all-gather.24
  194.9 57.6 all-gather.34
  253.9 57.6 all-gather.32
  312.9 57.6 all-gather.30
  372.1 57.6 all-gather.40
  431.3 57.6 all-gather.38
  490.5 57.6 all-gather.36
  608.7 57.6 all-gather.44
  667.7 57.6 all-gather.42
  727.9 122.6 reduce-scatter.34
  853.7 122.6 reduce-scatter.18
  978.8 122.6 reduce-scatter.26
  1104.0 122.6 reduce-scatter.32
  1229.7 122.6 reduce-scatter.16
  1354.8 122.6 reduce-scatter.24
  1480.1 122.6 reduce-scatter.30
  1605.8 122.6 reduce-scatter.14
  1731.1 122.6 reduce-scatter.22
  1856.4 122.6 reduce-scatter.28
  1981.7 122.6 reduce-scatter.12
  2106.9 122.6 reduce-scatter.20
  2233.2 1133.5 all-reduce.2
  (1 shorter events, 57.6 us)
where the time goes:
time: 3420 us; the launch traced here: 3410 us
  matrix products  1860 us (54%)
  waiting for transfers between devices  1380 us (40%)
  other arithmetic  128 us (4%)
    psum x1, waiting for transfers between devices, reduce_grad(): return lax.psum(shard_sum, 'dp')  1020 us
    dot_general x4, matrix products, layer_backward(): jnp.einsum('td,fd->tf', g_bf, down_w, preferred_element_type=jnp.float32)  389 us
    reduce_scatter x12, waiting for transfers between devices, reduce_grad(): lax.psum_scatter(local_grad, 'fsdp', scatter_dimension=0, tiled=True)  320 us
    dot_general x4, matrix products, layer_backward(): jnp.einsum('tf,td->fd', act_b, g_bf, preferred_element_type=jnp.float32)  280 us
    dot_general x4, matrix products, layer_backward(): jnp.einsum('tf,df->td', d_gate_b, gate_w, preferred_element_type=jnp.floa...  205 us
    dot_general x4, matrix products, layer_backward(): jnp.einsum('td,df->tf', norm_b, gate_w, preferred_element_type=jnp.float32)  202 us
    dot_general x4, matrix products, layer_backward(): jnp.einsum('tf,df->td', d_up_b, up_w, preferred_element_type=jnp.float32)  201 us
    dot_general x4, matrix products, layer_backward(): jnp.einsum('td,df->tf', norm_b, up_w, preferred_element_type=jnp.float32)  201 us
  transfers between devices with their start and end apart: 25, of which 6 were waited for; matrix products, arithmetic and copies ran while one was open for 58% of the time, Pallas kernels for 0%

commit v1 on v0

v1 whole, which is shorter than its diff:
```python
import functools

import jax
import jax.numpy as jnp
from jax import lax
from jax.experimental import pallas as pl
from jax.experimental.pallas import tpu as pltpu
from jax.sharding import PartitionSpec as P

EPS = 1e-5
MESH = pl.DeviceIdType.MESH
F32 = jnp.float32
BF16 = jnp.bfloat16
FB = 256
LEAD = 8
BASE = 240
DOT_NT = (((1,), (1,)), ((), ()))


def ring(i, n):
    return lax.rem(i + BASE, n)


def dot(a, b):
    return jnp.dot(a, b, preferred_element_type=F32)


def dot_nt(a, b):
    return lax.dot_general(a, b, DOT_NT, preferred_element_type=F32)


def kernel(
    dims, h_ref, g_ref, wgu_ref, wd_ref,
    dg_ref, du_ref, dd_ref, dh_ref, ggu, gwd, gt_ref,
    n_t, gb_t, dn_t, r_row, wgu_b, wd_b, w_t, s_a, s_du, s_dv, acc, hb,
    sg, sd, rdg, rdd, xsg, xsd, pog, pod, rxg, rxd, ysg, ysd, ryg, ryd, fog, fod,
    wl_sem, d_snd, d_rcv, x_snd, x_rcv, y_snd, y_rcv, o_sem, f_loc, f_snd, f_rcv,
    w_snd, w_rcv, hb_sem, gl_sem, gs_sem, do_sem,
):
    layers, tokens, width, hidden, tb, nb = dims
    dq = width // 4
    hq = dq // 2
    half = hidden // 2
    nj = hidden // FB
    mid = nj // 2
    steps = layers * nj
    y = lax.axis_index("dp")
    me = lax.axis_index("fsdp")
    x = me // 2
    c = me % 2
    qx = (1 - x) * 2 + c
    partner = (y, x * 2 + 1 - c)
    x_dev = (y, qx)
    y_dev = (1 - y, me)

    def layer_of(s):
        return layers - 1 - s // nj

    def block_of(t):
        return t // 2 + (t % 2) * (mid + 1)

    def owner_piece(t, e):
        last = t // (nj - 1)
        core = (1 - last) * (t % 2) + last * e
        piece = (1 - last) * (t + e) + last * (nj - 1) * (1 - e)
        return core, piece

    def remote(src, dst, snd, rcv, dev):
        return pltpu.make_async_remote_copy(
            src_ref=src, dst_ref=dst, send_sem=snd, recv_sem=rcv, device_id=dev, device_id_type=MESH
        )

    def weight_copies(kind, p):
        l, t = layer_of(p), p % nj
        rs = ring(p, 8)
        if kind in "AB":
            gu_src, wd_src, q = wgu_ref.at[l, block_of(t)], wd_ref.at[l, t], me
        else:
            gu_src, wd_src, q = ggu.at[p, qx], gwd.at[p, qx], qx
        gu_dst, wd_dst = ggu.at[p, q], gwd.at[p, q]
        if kind != "A":
            side = 1 - y if kind == "E" else y
            rows = pl.ds(pl.multiple_of(side * hq, 16), hq)
            rows_d = pl.ds(pl.multiple_of(side * 32, 32), 32)
            gu_src, gu_dst = gu_src.at[:, rows], gu_dst.at[:, rows]
            wd_src, wd_dst = wd_src.at[rows_d], wd_dst.at[rows_d]
        dev = {"A": partner, "B": x_dev, "C": y_dev, "D": partner, "E": partner}[kind]
        k = "ABCDE".index(kind)
        return (
            remote(gu_src, gu_dst, w_snd.at[k, 0, rs], w_rcv.at[k, 0, rs], dev),
            remote(wd_src, wd_dst, w_snd.at[k, 1, rs], w_rcv.at[k, 1, rs], dev),
        )

    def weight_start(kinds, p):
        @pl.when((p >= 0) & (p < steps))
        def _():
            for kind in kinds:
                for cp in weight_copies(kind, p):
                    cp.start()

    def weight_wait_recv(kinds, p):
        @pl.when((p >= 0) & (p < steps))
        def _():
            for kind in kinds:
                for cp in weight_copies(kind, p):
                    cp.wait_recv()

    def weight_wait_send(kinds, p):
        @pl.when((p >= 0) & (p < steps))
        def _():
            for kind in kinds:
                for cp in weight_copies(kind, p):
                    cp.wait_send()

    def load_weights(s, go):
        slot = ring(s, 2)
        l, t = layer_of(s), s % nj

        def act(src, dst, i):
            cp = pltpu.make_async_copy(src, dst, wl_sem.at[slot, i])
            cp.start() if go else cp.wait()

        for d in range(4):
            q = (me + d) % 4
            dst = wgu_b.at[slot, :, pl.ds(pl.multiple_of(q * dq, 16), dq)]
            act(wgu_ref.at[l, block_of(t)] if d == 0 else ggu.at[s, q], dst, d)
        for e in range(2):
            core, piece = owner_piece(t, e)
            for xx in range(2):
                q = xx * 2 + core
                dst = wd_b.at[slot, pl.ds(xx * 128 + e * 64, 64)]
                i = 4 + e * 2 + xx
                if go:
                    @pl.when(q == me)
                    def _():
                        act(wd_ref.at[l, piece], dst, i)

                    @pl.when(q != me)
                    def _():
                        act(gwd.at[s - t + piece, q], dst, i)
                else:
                    act(wd_ref.at[l, piece], dst, i)

    def core_copies(b):
        r, a, z = ring(b, 8), ring(b, 2), ring(b, 3)
        return (
            remote(sg.at[a, :, :, 1 - c], rdg.at[z], d_snd.at[0, r], d_rcv.at[0, r], partner),
            remote(sd.at[a, :, 1 - c], rdd.at[z], d_snd.at[1, r], d_rcv.at[1, r], partner),
        )

    def x_copies(b):
        r, a, z = ring(b, 8), ring(b, 3), ring(b, 5)
        return (
            remote(xsg.at[a], rxg.at[z], x_snd.at[0, r], x_rcv.at[0, r], x_dev),
            remote(xsd.at[a], rxd.at[z], x_snd.at[1, r], x_rcv.at[1, r], x_dev),
        )

    def y_copies(b):
        r, a, z = ring(b, 8), ring(b, 3), ring(b, 5)
        return (
            remote(ysg.at[a], ryg.at[z], y_snd.at[0, r], y_rcv.at[0, r], y_dev),
            remote(ysd.at[a], ryd.at[z], y_snd.at[1, r], y_rcv.at[1, r], y_dev),
        )

    def valid(b):
        return (b >= 0) & (b < steps)

    def start_all(copies, b):
        @pl.when(valid(b))
        def _():
            for cp in copies(b):
                cp.start()

    def wait_all(copies, b):
        @pl.when(valid(b))
        def _():
            for cp in copies(b):
                cp.wait_recv()
            for cp in copies(b):
                cp.wait_send()

    def out_gate_up(b):
        a = ring(b, 2)
        l, m = layer_of(b), block_of(b % nj)
        cps = []
        for gu, out in enumerate((dg_ref, du_ref)):
            for hf in range(2):
                cols = pl.ds(pl.multiple_of(hf * half + m * 128, 128), 128)
                src = fog.at[a, gu, :, pl.ds(hf * 128, 128)]
                cps.append(pltpu.make_async_copy(src, out.at[l, :, cols], o_sem.at[gu * 2 + hf, a]))
        return cps

    def out_down(b, own):
        a, r = ring(b, 2), ring(b, 4)
        core, piece = owner_piece(b % nj, c)
        dst = dd_ref.at[layer_of(b), pl.ds(pl.multiple_of(piece * 64, 64), 64)]
        if own:
            return pltpu.make_async_copy(fod.at[a], dst, f_loc.at[a])
        return remote(fod.at[a], dst, f_snd.at[r], f_rcv.at[r], partner)

    def out_start(b):
        @pl.when(valid(b))
        def _():
            for cp in out_gate_up(b):
                cp.start()
            core, _ = owner_piece(b % nj, c)

            @pl.when(core == c)
            def _():
                out_down(b, True).start()

            @pl.when(core != c)
            def _():
                out_down(b, False).start()

    def out_wait(b):
        @pl.when(valid(b))
        def _():
            for cp in out_gate_up(b):
                cp.wait()
            core, _ = owner_piece(b % nj, c)
            theirs, _ = owner_piece(b % nj, 1 - c)

            @pl.when(core == c)
            def _():
                out_down(b, True).wait()

            @pl.when(core != c)
            def _():
                out_down(b, False).wait_send()

            @pl.when(theirs == c)
            def _():
                out_down(b, False).wait_recv()

    def boundary(s):
        @pl.when((s >= 0) & (s < steps))
        def _():
            load_weights(s, False)

        wait_all(core_copies, s - 2)
        wait_all(x_copies, s - 5)
        wait_all(y_copies, s - 8)
        out_wait(s - 10)
        p = s + LEAD
        weight_wait_recv("B", p - 2)
        weight_wait_recv("C", p - 4)
        weight_wait_recv("ADE", p - 6)
        weight_wait_send("AB", p - 2)
        weight_wait_send("CD", p - 4)
        weight_wait_send("E", p - 6)
        weight_start("B", p)
        weight_start("A", p)
        weight_start("CD", p - 2)
        weight_start("E", p - 4)
        start_all(core_copies, s - 1)
        start_all(x_copies, s - 3)
        start_all(y_copies, s - 6)
        out_start(s - 9)

        @pl.when((s + 1 >= 0) & (s + 1 < steps))
        def _():
            load_weights(s + 1, True)

    def sums(s):
        a, b5, b3 = ring(s - 8, 2), ring(s - 8, 5), ring(s - 8, 3)
        for i in range(2):
            fog[a, i] = ysg[b3, i] + ryg[b5, i]
        fod[a] = ysd[b3] + ryd[b5]
        a, b5 = ring(s - 5, 3), ring(s - 5, 5)
        for i in range(2):
            ysg[a, i] = pog[a, i] + rxg[b5, i]
        ysd[a] = pod[a] + rxd[b5]
        a, b3 = ring(s - 2, 2), ring(s - 2, 3)
        for i in range(2):
            pog[b3, i] = sg[a, i, x, c] + rdg[b3, i, x]
            xsg[b3, i] = sg[a, i, 1 - x, c] + rdg[b3, i, 1 - x]
        pod[b3] = sd[a, x, c] + rdd[b3, x]
        xsd[b3] = sd[a, 1 - x, c] + rdd[b3, 1 - x]

    def compute(s):
        slot = ring(s, 2)
        for i in range(2):
            w_t[i] = wgu_b[slot, i].T
        blocks = tokens // tb

        def first(t):
            tok = pl.ds(t * tb, tb)
            u = dot(w_t[0], n_t[:, tok])
            v = dot(w_t[1], n_t[:, tok])
            da = dot(wd_b[slot], gb_t[:, tok])
            sig = jax.nn.sigmoid(u)
            silu = u * sig
            s_a[t % 2] = (silu * v).astype(BF16)
            s_du[t % 2] = (da * v * sig * (1.0 + u * (1.0 - sig))).astype(BF16)
            s_dv[t % 2] = (da * silu).astype(BF16)

        def second(t):
            tok = pl.ds(t * tb, tb)
            for i, val in enumerate((s_du, s_dv)):
                part = dot_nt(n_t[:, tok], val[t % 2])
                if t > 0:
                    part = acc[i] + part
                if t < blocks - 1:
                    acc[i] = part
                else:
                    sg[slot, i] = part.reshape(2, 2, dq, FB)
            part = dot_nt(gb_t[:, tok], s_a[t % 2])
            if t > 0:
                part = acc[2] + part
            if t < blocks - 1:
                acc[2] = part
            else:
                sd[slot] = part.T.reshape(2, 2, 64, width)
            dn_t[:, tok] += dot(wgu_b[slot, 0], s_du[t % 2]) + dot(wgu_b[slot, 1], s_dv[t % 2])

        first(0)
        for t in range(1, blocks):
            first(t)
            second(t - 1)
        second(blocks - 1)

    n_tok = tokens // nb

    def tok_of(i):
        return pl.ds(pl.multiple_of(i * nb, nb), nb)

    def rows_load(i, src, which):
        return pltpu.make_async_copy(src.at[tok_of(i)], hb.at[ring(i, 2), which], hb_sem.at[ring(i, 2), which])

    def g_load(i):
        return pltpu.make_async_copy(gt_ref.at[:, tok_of(i)], acc.at[ring(i, 3)], gl_sem.at[ring(i, 3)])

    def g_store(i):
        return pltpu.make_async_copy(acc.at[ring(i, 3)], gt_ref.at[:, tok_of(i)], gs_sem.at[ring(i, 3)])

    groups = [pl.ds(k, 128) for k in range(0, width, 128)]

    def new_norm(i):
        tok = tok_of(i)
        total = jnp.zeros((1, nb), F32)
        for rows in groups:
            xt = hb[ring(i, 2), 1, :, rows].T
            n_t[rows, tok] = xt
            xf = xt.astype(F32)
            total += jnp.sum(xf * xf, axis=0, keepdims=True)
        r = lax.rsqrt(total * (1.0 / width) + EPS)
        r_row[:, tok] = r
        for rows in groups:
            n_t[rows, tok] = (n_t[rows, tok].astype(F32) * r).astype(BF16)
            dn_t[rows, tok] = jnp.zeros((128, nb), F32)

    def new_g(i, put):
        tok = tok_of(i)
        r = r_row[:, tok]
        total = jnp.zeros((1, nb), F32)
        for rows in groups:
            xt = hb[ring(i, 2), 0, :, rows].T
            gb_t[rows, tok] = xt
            total += jnp.sum(dn_t[rows, tok] * (xt.astype(F32) * r), axis=0, keepdims=True)
        m = total * (1.0 / width)
        for rows in groups:
            nf = gb_t[rows, tok].astype(F32) * r
            put(rows, acc[ring(i, 3), rows] + r * (dn_t[rows, tok] - nf * m))

    def enter_block(i):
        h_new = h_ref.at[layers - 1]

        @pl.when(i == 0)
        def _():
            rows_load(i, g_ref, 0).start()
            rows_load(i, h_new, 1).start()

        @pl.when(i + 1 < n_tok)
        def _():
            rows_load(i + 1, g_ref, 0).start()
            rows_load(i + 1, h_new, 1).start()

        @pl.when(i >= 3)
        def _():
            g_store(i - 3).wait()

        rows_load(i, g_ref, 0).wait()
        rows_load(i, h_new, 1).wait()
        for rows in groups:
            gb = hb[ring(i, 2), 0, :, rows].T
            gb_t[rows, tok_of(i)] = gb
            acc[ring(i, 3), rows] = gb.astype(F32)
        new_norm(i)
        g_store(i).start()

    def stores_done():
        for i in range(n_tok - 3, n_tok):
            g_store(i).wait()

    def between(l_new):
        h_old, h_new = h_ref.at[l_new + 1], h_ref.at[l_new]
        rows_load(0, h_old, 0).start()
        rows_load(0, h_new, 1).start()
        g_load(0).start()

        def body(i, _):
            @pl.when(i >= 2)
            def _():
                g_store(i - 2).wait()

            @pl.when(i + 1 < n_tok)
            def _():
                rows_load(i + 1, h_old, 0).start()
                rows_load(i + 1, h_new, 1).start()
                g_load(i + 1).start()

            rows_load(i, h_old, 0).wait()
            rows_load(i, h_new, 1).wait()
            g_load(i).wait()

            def put(rows, g):
                acc[ring(i, 3), rows] = g
                gb_t[rows, tok_of(i)] = g.astype(BF16)

            new_g(i, put)
            new_norm(i)
            g_store(i).start()
            return 0

        lax.fori_loop(0, n_tok, body, 0)
        for i in range(n_tok - 2, n_tok):
            g_store(i).wait()

    def leave():
        h_old = h_ref.at[0]

        def dh_store(i):
            return pltpu.make_async_copy(hb.at[ring(i, 2), 1], dh_ref.at[tok_of(i)], do_sem.at[ring(i, 2)])

        rows_load(0, h_old, 0).start()
        g_load(0).start()

        def body(i, _):
            @pl.when(i + 1 < n_tok)
            def _():
                rows_load(i + 1, h_old, 0).start()
                g_load(i + 1).start()

            @pl.when(i >= 2)
            def _():
                dh_store(i - 2).wait()

            rows_load(i, h_old, 0).wait()
            g_load(i).wait()

            def put(rows, g):
                hb[ring(i, 2), 1, :, rows] = g.astype(BF16).T

            new_g(i, put)
            dh_store(i).start()
            return 0

        lax.fori_loop(0, n_tok, body, 0)
        for i in range(n_tok - 2, n_tok):
            dh_store(i).wait()

    barrier = pltpu.get_barrier_semaphore()
    for dev in (partner, x_dev, y_dev):
        pl.semaphore_signal(barrier, inc=1, device_id=dev, device_id_type=MESH)
    pl.semaphore_wait(barrier, 3)

    per = n_tok // LEAD

    def lead_in(i, _):
        boundary(i - LEAD)
        for k in range(per):
            enter_block(i * per + k)
        return 0

    lax.fori_loop(0, LEAD, lead_in, 0)
    stores_done()

    def main(s, _):
        boundary(s)

        @pl.when((s % nj == 0) & (s > 0))
        def _():
            between(layer_of(s))

        sums(s)
        compute(s)
        return 0

    lax.fori_loop(0, steps, main, 0)
    boundary(steps)
    sums(steps)
    leave()

    def drain(s, _):
        boundary(s)
        sums(s)
        return 0

    lax.fori_loop(steps + 1, steps + 10, drain, 0)


def backward(dims, h, g, wgu, wd):
    layers, tokens, width, hidden, tb, nb = dims
    dq = width // 4
    nj = hidden // FB
    steps = layers * nj
    dma = pltpu.SemaphoreType.DMA
    vm = pltpu.VMEM
    anyspace = pl.BlockSpec(memory_space=pl.ANY)
    sds = jax.ShapeDtypeStruct
    out_shape = [
        sds((layers, dq, hidden), F32),
        sds((layers, dq, hidden), F32),
        sds((layers, hidden // 4, width), F32),
        sds((tokens, width), BF16),
        sds((steps, 4, 2, dq, FB), BF16),
        sds((steps, 4, 64, width), BF16),
        sds((width, tokens), F32),
    ]

    def pair(n):
        return [vm((n, 2, dq, FB), F32), vm((n, 64, width), F32)]

    scratch = [
        vm((width, tokens), BF16),
        vm((width, tokens), BF16),
        vm((width, tokens), F32),
        vm((1, tokens), F32),
        vm((2, 2, width, FB), BF16),
        vm((2, FB, width), BF16),
        vm((2, FB, width), BF16),
        vm((2, FB, tb), BF16),
        vm((2, FB, tb), BF16),
        vm((2, FB, tb), BF16),
        vm((3, width, FB), F32),
        vm((2, 2, nb, width), BF16),
        vm((2, 2, 2, 2, dq, FB), F32),
        vm((2, 2, 2, 64, width), F32),
        vm((3, 2, 2, dq, FB), F32),
        vm((3, 2, 64, width), F32),
        *pair(3), *pair(3), *pair(5), *pair(3), *pair(5), *pair(2),
        dma((2, 8)),
        dma((2, 8)), dma((2, 8)), dma((2, 8)), dma((2, 8)), dma((2, 8)), dma((2, 8)),
        dma((4, 2)), dma((2,)), dma((4,)), dma((4,)),
        dma((5, 2, 8)), dma((5, 2, 8)),
        dma((2, 2)), dma((3,)), dma((3,)), dma((2,)),
    ]
    return pl.pallas_call(
        functools.partial(kernel, dims),
        out_shape=out_shape,
        in_specs=[anyspace] * 4,
        out_specs=[anyspace] * 7,
        scratch_shapes=scratch,
        compiler_params=pltpu.CompilerParams(
            collective_id=0, has_side_effects=True, vmem_limit_bytes=67043328
        ),
        name="mlp_backward",
    )(h, g, wgu, wd)[:4]


def solution(mesh):
    tok_spec = P(("dp", "fsdp"))
    stack_spec = P(None, ("dp", "fsdp"))
    weight_spec = P(None, "fsdp")

    def local_backward(h_saved, grad_out, gate_sh, up_sh, down_sh):
        layers = h_saved.shape[0]
        b_loc, seq, width = grad_out.shape
        tokens = b_loc * seq
        dq, hidden = gate_sh.shape[1:]
        nj = hidden // FB
        tb = min(256, tokens // 2)
        nb = FB
        wgu = jnp.stack([gate_sh, up_sh], axis=1).reshape(layers, 2, dq, 2, nj, 128)
        wgu = wgu.transpose(0, 4, 1, 2, 3, 5).reshape(layers, nj, 2, dq, FB)
        wd = down_sh.reshape(layers, nj, 64, width)
        dims = (layers, tokens, width, hidden, tb, nb)
        d_gate, d_up, d_down, d_h0 = backward(
            dims, h_saved.reshape(layers, tokens, width), grad_out.reshape(tokens, width), wgu, wd
        )
        return d_gate, d_up, d_down, d_h0.reshape(b_loc, seq, width)

    return jax.shard_map(
        local_backward,
        mesh=mesh,
        in_specs=(stack_spec, tok_spec, weight_spec, weight_spec, weight_spec),
        out_specs=(weight_spec, weight_spec, weight_spec, tok_spec),
        check_vma=False,
    )
```

time: 3420 us -> 1720 us (0.50)
  matrix products: 1860 us -> 0 us
  Pallas kernels: 0 us -> 1550 us
  waiting for transfers between devices: 1380 us -> 0 us
  local copies, waits for them, and re-layouts: 28.8 us -> 151 us
  other arithmetic: 128 us -> 17.3 us
    dot_general x32 -> x0, matrix products: 1860 us -> none  [the longest x4 389 us: layer_backward(): jnp.einsum('td,fd->tf', g_bf, down_w, preferred_element_type=jnp.float32)]
    pallas_call x0 -> x1, Pallas kernels: none -> 1550 us  [backward(): pl.pallas_call(functools.partial(kernel, dims), out_shape=out_shape, in_s...]
    psum x1 -> x0, waiting for transfers between devices: 1020 us -> none  [reduce_grad(): return lax.psum(shard_sum, 'dp')]
    reduce_scatter x12 -> x0, waiting for transfers between devices: 320 us -> none  [reduce_grad(): lax.psum_scatter(local_grad, 'fsdp', scatter_dimension=0, tiled=True)]
    add x3 -> x0, other arithmetic: 63.4 us -> none  [layer_backward(): return (g_acc + d_x, grad_gate, grad_up, grad_down)]
    unnamed x56 -> x22, local copies, waits for them, and re-layouts: 10.3 us -> 65.6 us
    transpose x0 -> x1, local copies, waits for them, and re-layouts: none -> 48 us  [local_backward(): wgu = wgu.transpose(0, 4, 1, 2, 3, 5).reshape(layers, nj, 2, dq, FB)]
    reshape x0 -> x1, local copies, waits for them, and re-layouts: none -> 37.7 us  [local_backward(): wgu = wgu.transpose(0, 4, 1, 2, 3, 5).reshape(layers, nj, 2, dq, FB)]
  transfers between devices with their start and end apart: 25 -> 0, of which waited for: 6 -> 0; matrix products, arithmetic and copies ran while one was open for 58% -> 0% of each run, Pallas kernels for 0% -> 0%
where the time goes in v1:
time: 1720 us; the launch traced here: 1710 us
  Pallas kernels  1550 us (90%)
  local copies, waits for them, and re-layouts  151 us (9%)
  other arithmetic  17.3 us (1%)
    pallas_call x1, Pallas kernels, backward(): pl.pallas_call(functools.partial(kernel, dims), out_shape=out_shape, in_s...  1550 us
    unnamed x22, local copies, waits for them, and re-layouts  65.6 us
    transpose x1, local copies, waits for them, and re-layouts, local_backward(): wgu = wgu.transpose(0, 4, 1, 2, 3, 5).reshape(layers, nj, 2, dq, FB)  48 us
    reshape x1, local copies, waits for them, and re-layouts, local_backward(): wgu = wgu.transpose(0, 4, 1, 2, 3, 5).reshape(layers, nj, 2, dq, FB)  37.7 us

profile of v1, /device:TPU:0, one launch (start us, length us, event | category | flops | bytes accessed | tf_op | source)
XLA Modules:
  0.0 1714.8 jit_solution(7132494170121831316)
XLA Ops:
  0.6 13.5 copy.11
  14.1 13.5 copy.12
  27.6 17.2 %maximum_bitcast_fusion = bf16[4,19,2,224,2,128]{3,5,1,4,0,2:T(8,128)(2,1)} fusion(bf16[4,1,224,2,19,128]{2,5,4,3,0,1:T(8,128)(2,1)} %bitcast.9, bf16[4,1,224,2,19,128]{2,5,4,3,0,1:T(8,128)(2,1)} %bitcast.8), kind=kLoop, calls=%fused_computation | loop fusion | flops 8716288 | bytes 34865152 | tf_op jit(solution)/shard_map/transpose | solution.py:576
  44.8 48.0 %copy.13 = bf16[4,19,2,224,2,128]{5,4,3,2,1,0:T(2,128)(2,1)} copy(bf16[4,19,2,224,2,128]{3,5,1,4,0,2:T(8,128)(2,1)} %maximum_bitcast_fusion) | data formatting | bytes 34865152 | tf_op jit(solution)/shard_map/transpose | solution.py:576
  92.8 37.7 %reshape.30.wgu_ref = bf16[4,19,2,224,256]{4,3,2,1,0:T(8,128)(2,1)} reshape(bf16[4,19,2,224,2,128]{5,4,3,2,1,0:T(2,128)(2,1)} %copy.13) | data formatting | bytes 34865152 | tf_op jit(solution)/shard_map/reshape | solution.py:576
  130.5 1545.6 %mlp_backward.1 = (f32[4,224,4864]{2,1,0:T(8,128)}, f32[4,224,4864]{2,1,0:T(8,128)}, f32[4,1216,896]{2,1,0:T(8,128)}, bf16[4096,896]{1,0:T(8,128)(2,1)}, bf16[76...) custom-call(bf16[4,4096,896]{2,1,0:T(8,128)(2,1)} %bitcast.10, ...), custom_call_target="tpu_custom_call" | custom-call | tf_op jit(solution)/shard_map/mlp_backward/pallas_call | solution.py:549
  1676.1 0.0 copy-start
  1676.1 0.0 slice-start
  1676.1 0.0 slice-start.1
  1676.1 0.0 slice-start.2
  1676.1 13.5 copy.18
  1689.7 3.5 copy-done
  1693.1 0.0 slice-start.3
  1693.1 0.0 slice-start.4
  1693.1 8.8 copy.19
  1702.0 0.0 slice-done
  1702.0 0.0 slice-done.1
  1702.0 1.0 slice-done.2
  1703.0 1.4 slice-done.3
  1704.4 0.1 slice-done.4
  1704.5 7.2 copy.20
  1711.7 0.0 slice-done.5
  1711.7 0.0 slice-done.6
  1711.7 3.0 copy.21
  (4 shorter events, 0.0 us)
Async XLA Ops:
  1676.1 17.0 copy-start
  1676.1 25.9 %slice-start = ((s8[17432576]{0:T(1024)(128)(4,1)}), s8[4194304]{0:T(1024)(128)(4,1)S(1)}, s32[]{:S(2)}) async-start(s8[17432576]{0:T(1024)(128)(4,1)} %bitcast.11), calls=%async_computation | async-start | bytes 8388608
  1676.1 25.8 %slice-start.1 = ((s8[17432576]{0:T(1024)(128)(4,1)}), s8[4194304]{0:T(1024)(128)(4,1)S(1)}, s32[]{:S(2)}) async-start(s8[17432576]{0:T(1024)(128)(4,1)} %bitcast.11), calls=%async_computation.1 | async-start | bytes 8388608
  1676.1 26.9 %slice-start.2 = ((s8[17432576]{0:T(1024)(128)(4,1)}), s8[4194304]{0:T(1024)(128)(4,1)S(1)}, s32[]{:S(2)}) async-start(s8[17432576]{0:T(1024)(128)(4,1)} %bitcast.11), calls=%async_computation.2 | async-start | bytes 8388608
  1693.1 11.3 slice-start.3
  1693.1 11.4 slice-start.4
  1693.1 18.6 %slice-start.5 = ((s8[7340032]{0:T(1024)(128)(4,1)}), s8[3145728]{0:T(1024)(128)(4,1)S(1)}, s32[]{:S(2)}) async-start(s8[7340032]{0:T(1024)(128)(4,1)} %bitcast.15), calls=%async_computation.5 | async-start | bytes 6291456
  1704.5 7.2 slice-start.6

commit v2 on v1

--- a/solution.py
+++ b/solution.py
@@ -13,12 +13,22 @@
 BF16 = jnp.bfloat16
 FB = 256
 LEAD = 8
+BURST = 6
+RS = 32
 BASE = 240
 DOT_NT = (((1,), (1,)), ((), ()))
 
 
+def div(a, b):
+    return a // b if isinstance(a, int) else lax.div(a, jnp.int32(b))
+
+
+def rem(a, b):
+    return a % b if isinstance(a, int) else lax.rem(a, jnp.int32(b))
+
+
 def ring(i, n):
-    return lax.rem(i + BASE, n)
+    return rem(i + BASE, n)
 
 
 def dot(a, b):
@@ -30,14 +40,14 @@
 
 
 def kernel(
-    dims, h_ref, g_ref, wgu_ref, wd_ref,
+    dims, h_ref, g_ref, gate_ref, up_ref, wd_ref,
     dg_ref, du_ref, dd_ref, dh_ref, ggu, gwd, gt_ref,
-    n_t, gb_t, dn_t, r_row, wgu_b, wd_b, w_t, s_a, s_du, s_dv, acc, hb,
+    n_t, gb_t, dn_t, r_row, wgu_b, wd_b, s_a, s_du, s_dv, acc, hb,
     sg, sd, rdg, rdd, xsg, xsd, pog, pod, rxg, rxd, ysg, ysd, ryg, ryd, fog, fod,
     wl_sem, d_snd, d_rcv, x_snd, x_rcv, y_snd, y_rcv, o_sem, f_loc, f_snd, f_rcv,
     w_snd, w_rcv, hb_sem, gl_sem, gs_sem, do_sem,
 ):
-    layers, tokens, width, hidden, tb, nb = dims
+    layers, tokens, width, hidden, tb, sub, nb = dims
     dq = width // 4
     hq = dq // 2
     half = hidden // 2
@@ -54,14 +64,14 @@
     y_dev = (1 - y, me)
 
     def layer_of(s):
-        return layers - 1 - s // nj
+        return layers - 1 - div(s, nj)
 
     def block_of(t):
-        return t // 2 + (t % 2) * (mid + 1)
+        return div(t, 2) + rem(t, 2) * (mid + 1)
 
     def owner_piece(t, e):
-        last = t // (nj - 1)
-        core = (1 - last) * (t % 2) + last * e
+        last = div(t, nj - 1)
+        core = (1 - last) * rem(t, 2) + last * e
         piece = (1 - last) * (t + e) + last * (nj - 1) * (1 - e)
         return core, piece
 
@@ -70,60 +80,101 @@
             src_ref=src, dst_ref=dst, send_sem=snd, recv_sem=rcv, device_id=dev, device_id_type=MESH
         )
 
-    def weight_copies(kind, p):
-        l, t = layer_of(p), p % nj
-        rs = ring(p, 8)
-        if kind in "AB":
-            gu_src, wd_src, q = wgu_ref.at[l, block_of(t)], wd_ref.at[l, t], me
+    def next_piece(beta, n):
+        burst = ((beta >= LEAD) & (beta < LEAD + 3)).astype(jnp.int32)
+        skip = ((beta >= LEAD + 3) & (rem(beta, 6) == 4)).astype(jnp.int32)
+        return n + (1 + (BURST - 1) * burst - skip) * (n < steps).astype(jnp.int32)
+
+    def shard_parts(l, t, rows):
+        m = block_of(t)
+        for gu, ref in enumerate((gate_ref, up_ref)):
+            for hf in range(2):
+                cols = pl.ds(pl.multiple_of(hf * half + m * 128, 128), 128)
+                yield ref.at[l, rows, cols], gu, pl.ds(hf * 128, 128)
+
+    def weight_copies(kind, p, whole):
+        l, t = layer_of(p), rem(p, nj)
+        rs = ring(p, RS)
+        k = "ABCDE".index(kind)
+        q = me if kind in "AB" else qx
+        dev = {"A": partner, "B": x_dev, "C": y_dev, "D": partner, "E": partner}[kind]
+        if kind == "A":
+            rows, rows_d = pl.ds(0, dq), pl.ds(0, 64)
         else:
-            gu_src, wd_src, q = ggu.at[p, qx], gwd.at[p, qx], qx
-        gu_dst, wd_dst = ggu.at[p, q], gwd.at[p, q]
-        if kind != "A":
             side = 1 - y if kind == "E" else y
             rows = pl.ds(pl.multiple_of(side * hq, 16), hq)
             rows_d = pl.ds(pl.multiple_of(side * 32, 32), 32)
-            gu_src, gu_dst = gu_src.at[:, rows], gu_dst.at[:, rows]
-            wd_src, wd_dst = wd_src.at[rows_d], wd_dst.at[rows_d]
-        dev = {"A": partner, "B": x_dev, "C": y_dev, "D": partner, "E": partner}[kind]
-        k = "ABCDE".index(kind)
-        return (
-            remote(gu_src, gu_dst, w_snd.at[k, 0, rs], w_rcv.at[k, 0, rs], dev),
-            remote(wd_src, wd_dst, w_snd.at[k, 1, rs], w_rcv.at[k, 1, rs], dev),
-        )
+        sems = w_snd.at[k, 0, rs], w_rcv.at[k, 0, rs]
+        if kind in "AB" and not whole:
+            for src, gu, lanes in shard_parts(l, t, rows):
+                yield remote(src, ggu.at[p, q, gu, rows, lanes], *sems, dev)
+        else:
+            both = ggu.at[p, q, :, rows]
+            yield remote(both, both, *sems, dev)
+        wd_dst = gwd.at[p, q, rows_d]
+        wd_src = wd_ref.at[l, t, rows_d] if kind in "AB" else wd_dst
+        yield remote(wd_src, wd_dst, w_snd.at[k, 1, rs], w_rcv.at[k, 1, rs], dev)
+
+    def pieces(span, act):
+        def body(p, _):
+            act(p)
+            return 0
+
+        lax.fori_loop(*span, body, 0)
 
     def weight_start(kinds, p):
-        @pl.when((p >= 0) & (p < steps))
-        def _():
-            for kind in kinds:
-                for cp in weight_copies(kind, p):
-                    cp.start()
+        for kind in kinds:
+            for cp in weight_copies(kind, p, False):
+                cp.start()
 
     def weight_wait_recv(kinds, p):
-        @pl.when((p >= 0) & (p < steps))
-        def _():
-            for kind in kinds:
-                for cp in weight_copies(kind, p):
-                    cp.wait_recv()
+        for kind in kinds:
+            for cp in weight_copies(kind, p, True):
+                cp.wait_recv()
 
     def weight_wait_send(kinds, p):
-        @pl.when((p >= 0) & (p < steps))
-        def _():
-            for kind in kinds:
-                for cp in weight_copies(kind, p):
-                    cp.wait_send()
+        for kind in kinds:
+            for cp in weight_copies(kind, p, True):
+                cp.wait_send()
+
+    def weights_wait(sent):
+        def arrived_x(p):
+            weight_wait_recv("B", p)
+            weight_wait_send("AB", p)
+
+        def arrived_y(p):
+            weight_wait_recv("C", p)
+            weight_wait_send("CD", p)
+
+        def complete(p):
+            weight_wait_recv("ADE", p)
+            weight_wait_send("E", p)
+
+        pieces((sent[3], sent[2]), arrived_x)
+        pieces((sent[5], sent[4]), arrived_y)
+        pieces((sent[7], sent[6]), complete)
+
+    def weights_send(sent):
+        pieces((sent[1], sent[0]), functools.partial(weight_start, "BA"))
+        pieces((sent[3], sent[2]), functools.partial(weight_start, "CD"))
+        pieces((sent[5], sent[4]), functools.partial(weight_start, "E"))
 
     def load_weights(s, go):
         slot = ring(s, 2)
-        l, t = layer_of(s), s % nj
+        l, t = layer_of(s), rem(s, nj)
 
         def act(src, dst, i):
             cp = pltpu.make_async_copy(src, dst, wl_sem.at[slot, i])
             cp.start() if go else cp.wait()
 
         for d in range(4):
-            q = (me + d) % 4
-            dst = wgu_b.at[slot, :, pl.ds(pl.multiple_of(q * dq, 16), dq)]
-            act(wgu_ref.at[l, block_of(t)] if d == 0 else ggu.at[s, q], dst, d)
+            q = rem(me + d, 4)
+            rows = pl.ds(pl.multiple_of(q * dq, 16), dq)
+            if d == 0 and go:
+                for src, gu, lanes in shard_parts(l, t, pl.ds(0, dq)):
+                    act(src, wgu_b.at[slot, gu, rows, lanes], d)
+            else:
+                act(ggu.at[s, q], wgu_b.at[slot, :, rows], d)
         for e in range(2):
             core, piece = owner_piece(t, e)
             for xx in range(2):
@@ -142,21 +193,21 @@
                     act(wd_ref.at[l, piece], dst, i)
 
     def core_copies(b):
-        r, a, z = ring(b, 8), ring(b, 2), ring(b, 3)
+        r, a, z = ring(b, 8), ring(b, 2), ring(b, 2)
         return (
             remote(sg.at[a, :, :, 1 - c], rdg.at[z], d_snd.at[0, r], d_rcv.at[0, r], partner),
             remote(sd.at[a, :, 1 - c], rdd.at[z], d_snd.at[1, r], d_rcv.at[1, r], partner),
         )
 
     def x_copies(b):
-        r, a, z = ring(b, 8), ring(b, 3), ring(b, 5)
+        r, a, z = ring(b, 8), ring(b, 2), ring(b, 4)
         return (
             remote(xsg.at[a], rxg.at[z], x_snd.at[0, r], x_rcv.at[0, r], x_dev),
             remote(xsd.at[a], rxd.at[z], x_snd.at[1, r], x_rcv.at[1, r], x_dev),
         )
 
     def y_copies(b):
-        r, a, z = ring(b, 8), ring(b, 3), ring(b, 5)
+        r, a, z = ring(b, 8), ring(b, 2), ring(b, 4)
         return (
             remote(ysg.at[a], ryg.at[z], y_snd.at[0, r], y_rcv.at[0, r], y_dev),
             remote(ysd.at[a], ryd.at[z], y_snd.at[1, r], y_rcv.at[1, r], y_dev),
@@ -181,7 +232,7 @@
 
     def out_gate_up(b):
         a = ring(b, 2)
-        l, m = layer_of(b), block_of(b % nj)
+        l, m = layer_of(b), block_of(rem(b, nj))
         cps = []
         for gu, out in enumerate((dg_ref, du_ref)):
             for hf in range(2):
@@ -191,8 +242,8 @@
         return cps
 
     def out_down(b, own):
-        a, r = ring(b, 2), ring(b, 4)
-        core, piece = owner_piece(b % nj, c)
+        a, r = ring(b, 2), ring(b, 8)
+        core, piece = owner_piece(rem(b, nj), c)
         dst = dd_ref.at[layer_of(b), pl.ds(pl.multiple_of(piece * 64, 64), 64)]
         if own:
             return pltpu.make_async_copy(fod.at[a], dst, f_loc.at[a])
@@ -203,7 +254,7 @@
         def _():
             for cp in out_gate_up(b):
                 cp.start()
-            core, _ = owner_piece(b % nj, c)
+            core, _ = owner_piece(rem(b, nj), c)
 
             @pl.when(core == c)
             def _():
@@ -218,8 +269,8 @@
         def _():
             for cp in out_gate_up(b):
                 cp.wait()
-            core, _ = owner_piece(b % nj, c)
-            theirs, _ = owner_piece(b % nj, 1 - c)
+            core, _ = owner_piece(rem(b, nj), c)
+            theirs, _ = owner_piece(rem(b, nj), 1 - c)
 
             @pl.when(core == c)
             def _():
@@ -233,92 +284,108 @@
             def _():
                 out_down(b, False).wait_recv()
 
-    def boundary(s):
+    def sum_y(b):
+        a, z = ring(b, 2), ring(b, 4)
+        for i in range(2):
+            fog[a, i] = ysg[a, i] + ryg[z, i]
+        fod[a] = ysd[a] + ryd[z]
+
+    def sum_x(b):
+        a, z = ring(b, 2), ring(b, 4)
+        for i in range(2):
+            ysg[a, i] = pog[a, i] + rxg[z, i]
+        ysd[a] = pod[a] + rxd[z]
+
+    def sum_cores(b):
+        a = ring(b, 2)
+        for i in range(2):
+            pog[a, i] = sg[a, i, x, c] + rdg[a, i, x]
+            xsg[a, i] = sg[a, i, 1 - x, c] + rdg[a, i, 1 - x]
+        pod[a] = sd[a, x, c] + rdd[a, x]
+        xsd[a] = sd[a, 1 - x, c] + rdd[a, 1 - x]
+
+    def sums(s):
+        @pl.when((s >= 6) & (s < steps + 2))
+        def _():
+            sum_y(s - 6)
+            sum_x(s - 4)
+            sum_cores(s - 2)
+
+        for f, b, alone in ((sum_y, s - 6, s >= steps + 2), (sum_x, s - 4, (s < 6) | (s >= steps + 2)),
+                            (sum_cores, s - 2, s < 6)):
+            @pl.when(valid(b) & alone)
+            def _():
+                f(b)
+
+    def boundary(s, sent):
+        sent = (next_piece(s + LEAD, sent[0]), *sent[:-1])
+
         @pl.when((s >= 0) & (s < steps))
         def _():
             load_weights(s, False)
 
         wait_all(core_copies, s - 2)
-        wait_all(x_copies, s - 5)
-        wait_all(y_copies, s - 8)
-        out_wait(s - 10)
-        p = s + LEAD
-        weight_wait_recv("B", p - 2)
-        weight_wait_recv("C", p - 4)
-        weight_wait_recv("ADE", p - 6)
-        weight_wait_send("AB", p - 2)
-        weight_wait_send("CD", p - 4)
-        weight_wait_send("E", p - 6)
-        weight_start("B", p)
-        weight_start("A", p)
-        weight_start("CD", p - 2)
-        weight_start("E", p - 4)
+        wait_all(x_copies, s - 4)
+        wait_all(y_copies, s - 6)
+        out_wait(s - 8)
+        sums(s)
+        weights_wait(sent)
+        weights_send(sent)
+
+        @pl.when((s + 1 >= 0) & (s + 1 < steps))
+        def _():
+            load_weights(s + 1, True)
+
         start_all(core_copies, s - 1)
-        start_all(x_copies, s - 3)
-        start_all(y_copies, s - 6)
-        out_start(s - 9)
-
-        @pl.when((s + 1 >= 0) & (s + 1 < steps))
-        def _():
-            load_weights(s + 1, True)
-
-    def sums(s):
-        a, b5, b3 = ring(s - 8, 2), ring(s - 8, 5), ring(s - 8, 3)
-        for i in range(2):
-            fog[a, i] = ysg[b3, i] + ryg[b5, i]
-        fod[a] = ysd[b3] + ryd[b5]
-        a, b5 = ring(s - 5, 3), ring(s - 5, 5)
-        for i in range(2):
-            ysg[a, i] = pog[a, i] + rxg[b5, i]
-        ysd[a] = pod[a] + rxd[b5]
-        a, b3 = ring(s - 2, 2), ring(s - 2, 3)
-        for i in range(2):
-            pog[b3, i] = sg[a, i, x, c] + rdg[b3, i, x]
-            xsg[b3, i] = sg[a, i, 1 - x, c] + rdg[b3, i, 1 - x]
-        pod[b3] = sd[a, x, c] + rdd[b3, x]
-        xsd[b3] = sd[a, 1 - x, c] + rdd[b3, 1 - x]
+        start_all(x_copies, s - 2)
+        start_all(y_copies, s - 4)
+        out_start(s - 6)
+        return sent
 
     def compute(s):
         slot = ring(s, 2)
         for i in range(2):
-            w_t[i] = wgu_b[slot, i].T
-        blocks = tokens // tb
+            hb[0, i] = wgu_b[slot, i].T
+        fine = tokens // tb
+        coarse = fine // sub
 
         def first(t):
             tok = pl.ds(t * tb, tb)
-            u = dot(w_t[0], n_t[:, tok])
-            v = dot(w_t[1], n_t[:, tok])
+            u = dot(hb[0, 0], n_t[:, tok])
+            v = dot(hb[0, 1], n_t[:, tok])
             da = dot(wd_b[slot], gb_t[:, tok])
             sig = jax.nn.sigmoid(u)
             silu = u * sig
-            s_a[t % 2] = (silu * v).astype(BF16)
-            s_du[t % 2] = (da * v * sig * (1.0 + u * (1.0 - sig))).astype(BF16)
-            s_dv[t % 2] = (da * silu).astype(BF16)
+            at = (t // sub) % 2, slice(None), pl.ds((t % sub) * tb, tb)
+            s_a[at] = (silu * v).astype(BF16)
+            s_du[at] = (da * v * sig * (1.0 + u * (1.0 - sig))).astype(BF16)
+            s_dv[at] = (da * silu).astype(BF16)
 
         def second(t):
-            tok = pl.ds(t * tb, tb)
+            tok = pl.ds(t * tb * sub, tb * sub)
             for i, val in enumerate((s_du, s_dv)):
                 part = dot_nt(n_t[:, tok], val[t % 2])
                 if t > 0:
                     part = acc[i] + part
-                if t < blocks - 1:
+                if t < coarse - 1:
                     acc[i] = part
                 else:
                     sg[slot, i] = part.reshape(2, 2, dq, FB)
             part = dot_nt(gb_t[:, tok], s_a[t % 2])
             if t > 0:
                 part = acc[2] + part
-            if t < blocks - 1:
+            if t < coarse - 1:
                 acc[2] = part
             else:
                 sd[slot] = part.T.reshape(2, 2, 64, width)
             dn_t[:, tok] += dot(wgu_b[slot, 0], s_du[t % 2]) + dot(wgu_b[slot, 1], s_dv[t % 2])
 
-        first(0)
-        for t in range(1, blocks):
-            first(t)
-            second(t - 1)
-        second(blocks - 1)
+        for t in range(coarse):
+            for k in range(sub):
+                first(t * sub + k)
+            if t:
+                second(t - 1)
+        second(coarse - 1)
 
     n_tok = tokens // nb
 
@@ -467,41 +534,33 @@
 
     per = n_tok // LEAD
 
-    def lead_in(i, _):
-        boundary(i - LEAD)
+    def lead_in(i, sent):
+        sent = boundary(i - LEAD, sent)
         for k in range(per):
             enter_block(i * per + k)
-        return 0
-
-    lax.fori_loop(0, LEAD, lead_in, 0)
+        return sent
+
+    sent = lax.fori_loop(0, LEAD, lead_in, (jnp.int32(0),) * 8)
     stores_done()
 
-    def main(s, _):
-        boundary(s)
-
-        @pl.when((s % nj == 0) & (s > 0))
+    def main(s, sent):
+        sent = boundary(s, sent)
+
+        @pl.when((rem(s, nj) == 0) & (s > 0))
         def _():
             between(layer_of(s))
 
-        sums(s)
         compute(s)
-        return 0
-
-    lax.fori_loop(0, steps, main, 0)
-    boundary(steps)
-    sums(steps)
+        return sent
+
+    sent = lax.fori_loop(0, steps, main, sent)
+    sent = boundary(jnp.int32(steps), sent)
     leave()
-
-    def drain(s, _):
-        boundary(s)
-        sums(s)
-        return 0
-
-    lax.fori_loop(steps + 1, steps + 10, drain, 0)
-
-
-def backward(dims, h, g, wgu, wd):
-    layers, tokens, width, hidden, tb, nb = dims
+    lax.fori_loop(steps + 1, steps + 8, boundary, sent)
+
+
+def backward(dims, h, g, gate, up, wd):
+    layers, tokens, width, hidden, tb, sub, nb = dims
     dq = width // 4
     nj = hidden // FB
     steps = layers * nj
@@ -529,34 +588,33 @@
         vm((1, tokens), F32),
         vm((2, 2, width, FB), BF16),
         vm((2, FB, width), BF16),
-        vm((2, FB, width), BF16),
-        vm((2, FB, tb), BF16),
-        vm((2, FB, tb), BF16),
-        vm((2, FB, tb), BF16),
+        vm((2, FB, tb * sub), BF16),
+        vm((2, FB, tb * sub), BF16),
+        vm((2, FB, tb * sub), BF16),
         vm((3, width, FB), F32),
         vm((2, 2, nb, width), BF16),
         vm((2, 2, 2, 2, dq, FB), F32),
         vm((2, 2, 2, 64, width), F32),
-        vm((3, 2, 2, dq, FB), F32),
-        vm((3, 2, 64, width), F32),
-        *pair(3), *pair(3), *pair(5), *pair(3), *pair(5), *pair(2),
+        vm((2, 2, 2, dq, FB), F32),
+        vm((2, 2, 64, width), F32),
+        *pair(2), *pair(2), *pair(4), *pair(2), *pair(4), *pair(2),
         dma((2, 8)),
         dma((2, 8)), dma((2, 8)), dma((2, 8)), dma((2, 8)), dma((2, 8)), dma((2, 8)),
-        dma((4, 2)), dma((2,)), dma((4,)), dma((4,)),
-        dma((5, 2, 8)), dma((5, 2, 8)),
+        dma((4, 2)), dma((2,)), dma((8,)), dma((8,)),
+        dma((5, 2, RS)), dma((5, 2, RS)),
         dma((2, 2)), dma((3,)), dma((3,)), dma((2,)),
     ]
     return pl.pallas_call(
         functools.partial(kernel, dims),
         out_shape=out_shape,
-        in_specs=[anyspace] * 4,
+        in_specs=[anyspace] * 5,
         out_specs=[anyspace] * 7,
         scratch_shapes=scratch,
         compiler_params=pltpu.CompilerParams(
             collective_id=0, has_side_effects=True, vmem_limit_bytes=67043328
         ),
         name="mlp_backward",
-    )(h, g, wgu, wd)[:4]
+    )(h, g, gate, up, wd)[:4]
 
 
 def solution(mesh):
@@ -570,14 +628,13 @@
         tokens = b_loc * seq
         dq, hidden = gate_sh.shape[1:]
         nj = hidden // FB
-        tb = min(256, tokens // 2)
+        tb = min(512, tokens // 2)
         nb = FB
-        wgu = jnp.stack([gate_sh, up_sh], axis=1).reshape(layers, 2, dq, 2, nj, 128)
-        wgu = wgu.transpose(0, 4, 1, 2, 3, 5).reshape(layers, nj, 2, dq, FB)
         wd = down_sh.reshape(layers, nj, 64, width)
-        dims = (layers, tokens, width, hidden, tb, nb)
+        sub = 1
+        dims = (layers, tokens, width, hidden, tb, sub, nb)
         d_gate, d_up, d_down, d_h0 = backward(
-            dims, h_saved.reshape(layers, tokens, width), grad_out.reshape(tokens, width), wgu, wd
+            dims, h_saved.reshape(layers, tokens, width), grad_out.reshape(tokens, width), gate_sh, up_sh, wd
         )
         return d_gate, d_up, d_down, d_h0.reshape(b_loc, seq, width)
 

time: 1720 us -> 1560 us (0.907)
  local copies, waits for them, and re-layouts: 151 us -> 38.6 us
  Pallas kernels: 1550 us -> 1520 us
  other arithmetic: 17.3 us -> 0.01 us
    transpose x1 -> x0, local copies, waits for them, and re-layouts: 48 us -> none  [local_backward(): wgu = wgu.transpose(0, 4, 1, 2, 3, 5).reshape(layers, nj, 2, dq, FB)]
    reshape x1 -> x0, local copies, waits for them, and re-layouts: 37.7 us -> none  [local_backward(): wgu = wgu.transpose(0, 4, 1, 2, 3, 5).reshape(layers, nj, 2, dq, FB)]
    unnamed x22 -> x20, local copies, waits for them, and re-layouts: 65.6 us -> 38.6 us
    pallas_call x1, Pallas kernels: 1550 us -> 1520 us  [backward(): pl.pallas_call(functools.partial(kernel, dims), out_shape=out_shape, in_s...]
    transpose x1 -> x0, other arithmetic: 17.2 us -> none  [local_backward(): wgu = wgu.transpose(0, 4, 1, 2, 3, 5).reshape(layers, nj, 2, dq, FB)]
where the time goes in v2:
time: 1560 us
  Pallas kernels  1520 us (97%)
  local copies, waits for them, and re-layouts  38.6 us (2%)
    pallas_call x1, Pallas kernels, backward(): pl.pallas_call(functools.partial(kernel, dims), out_shape=out_shape, in_s...  1520 us
    unnamed x20, local copies, waits for them, and re-layouts  38.6 us

profile of v2, /device:TPU:0, one launch (start us, length us, event | category | flops | bytes accessed | tf_op | source)
XLA Modules:
  0.0 1560.1 jit_solution(5619952513268620100)
XLA Ops:
  0.6 1520.8 %mlp_backward.1 = (f32[4,224,4864]{2,1,0:T(8,128)}, f32[4,224,4864]{2,1,0:T(8,128)}, f32[4,1216,896]{2,1,0:T(8,128)}, bf16[4096,896]{1,0:T(8,128)(2,1)}, bf16[76...) custom-call(bf16[4,4096,896]{2,1,0:T(8,128)(2,1)} %bitcast.4, ...), custom_call_target="tpu_custom_call" | custom-call | tf_op jit(solution)/shard_map/mlp_backward/pallas_call | solution.py:607
  1521.5 0.0 copy-start
  1521.5 0.0 slice-start
  1521.5 0.0 slice-start.1
  1521.5 0.0 slice-start.2
  1521.5 13.5 copy.13
  1535.0 3.5 copy-done
  1538.5 0.0 slice-start.3
  1538.5 0.0 slice-start.4
  1538.5 0.0 slice-start.5
  1538.5 8.8 copy.14
  1547.3 0.0 slice-done
  1547.3 0.0 slice-done.1
  1547.3 1.0 slice-done.2
  1548.4 1.4 slice-done.3
  1549.8 0.1 slice-done.4
  1549.9 0.0 slice-start.6
  1549.9 7.2 copy.15
  1557.1 0.0 slice-done.5
  1557.1 0.0 slice-done.6
  1557.1 3.0 copy.16
  (2 shorter events, 0.0 us)
Async XLA Ops:
  1521.5 17.0 %copy-start = (f32[4,224,4864]{2,1,0:T(8,128)S(1)}, f32[4,224,4864]{2,1,0:T(8,128)}, u32[]{:S(2)}) copy-start(f32[4,224,4864]{2,1,0:T(8,128)} %get-tuple-element.17) | copy-start | bytes 52297732
  1521.5 25.9 %slice-start = ((s8[17432576]{0:T(1024)(128)(4,1)}), s8[4194304]{0:T(1024)(128)(4,1)S(1)}, s32[]{:S(2)}) async-start(s8[17432576]{0:T(1024)(128)(4,1)} %bitcast.5), calls=%async_computation | async-start | bytes 8388608
  1521.5 25.8 %slice-start.1 = ((s8[17432576]{0:T(1024)(128)(4,1)}), s8[4194304]{0:T(1024)(128)(4,1)S(1)}, s32[]{:S(2)}) async-start(s8[17432576]{0:T(1024)(128)(4,1)} %bitcast.5), calls=%async_computation.1 | async-start | bytes 8388608
  1521.5 26.9 %slice-start.2 = ((s8[17432576]{0:T(1024)(128)(4,1)}), s8[4194304]{0:T(1024)(128)(4,1)S(1)}, s32[]{:S(2)}) async-start(s8[17432576]{0:T(1024)(128)(4,1)} %bitcast.5), calls=%async_computation.2 | async-start | bytes 8388608
  1538.5 11.3 slice-start.3
  1538.5 11.4 slice-start.4
  1538.5 18.6 %slice-start.5 = ((s8[7340032]{0:T(1024)(128)(4,1)}), s8[3145728]{0:T(1024)(128)(4,1)S(1)}, s32[]{:S(2)}) async-start(s8[7340032]{0:T(1024)(128)(4,1)} %bitcast.9), calls=%async_computation.5 | async-start | bytes 6291456
  1549.9 7.2 slice-start.6
